TPU v7x, 256 devices: a whole 4x4x8 slice. The times are simulated.
256 devices in a mesh: ep: 8 (over y, core), fsdp: 32 (over z, x).
Axes of the slice: x: 4, y: 4, z: 8, core: 2. Of those that a mesh axis runs over, the one named last changes fastest.
Arguments:
- w_down: float32 [16, 6400, 4096], P('ep', None, 'fsdp'), may hold values from -0.15625 to 0.15625
- router_weight: float32 [4096, 16], P('fsdp', 'ep'), may hold values from -0.09375 to 0.09375
- router_gain: float32 [4096], P('fsdp'), may hold values from 0.25 to 1.75
Outputs:
- serve_down: bfloat16 [16, 6400, 4096], P('ep', 'fsdp')
- scale_down: float32 [16, 6400], P('ep', 'fsdp')
- serve_router: bfloat16 [4096, 16], replicated
All inputs are finite; a program needn't handle non-finite values.
Results may differ from a plain program's by a relative error of at most 0.001.
Values may be sent and summed in bfloat16 or wider, within the bound.
A program may use at most 64 MiB of HBM per device.

v0:
```python
import jax
import jax.numpy as jnp
from jax import lax
from jax.sharding import Mesh
from jax.sharding import PartitionSpec as P

FSDP = ("fsdp_0", "fsdp_1")


def by_axis(array, axes):
    for axis in axes:
        array = lax.psum(array, axis)
    return array


def in_order(parts, dim):
    lengths = list(parts.shape[1:])
    lengths[dim] *= parts.shape[0]
    return jnp.moveaxis(parts, 0, dim).reshape(lengths)


def copy_for_each(array, axis):
    size = lax.axis_size(axis)
    return lax.all_to_all(
        jnp.broadcast_to(array[None], (size, *array.shape)), axis, 0, 0, tiled=True
    )


def gather_directly(array, axis, dim):
    return in_order(copy_for_each(array, axis), dim)


def body(w_down, router_weight, router_gain):
    total_down = by_axis(jnp.sum(w_down * w_down, axis=2), FSDP)
    scale_down = jnp.sqrt(total_down)
    narrow_down = (w_down / jnp.expand_dims(scale_down, 2)).astype(jnp.bfloat16)
    serve_down = lax.all_to_all(narrow_down, FSDP, split_axis=1, concat_axis=2, tiled=True)
    scale_down = lax.dynamic_slice_in_dim(
        scale_down, lax.axis_index(FSDP) * serve_down.shape[1], serve_down.shape[1], axis=1
    )
    part_router = (router_weight * router_gain[:, None]).astype(jnp.bfloat16)
    row_router = gather_directly(part_router, FSDP, 0)
    serve_router = lax.all_gather(row_router, "ep", axis=1, tiled=True)
    return (serve_down, scale_down, serve_router)


def solution(mesh):
    split = Mesh(mesh.devices.reshape(mesh.shape["ep"], 8, 4), ("ep", "fsdp_0", "fsdp_1"))
    return jax.shard_map(
        body,
        mesh=split,
        in_specs=(P("ep", None, FSDP), P(FSDP, "ep"), P(FSDP)),
        out_specs=(P("ep", FSDP, None), P("ep", FSDP), P()),
        check_vma=False,
    )
```

profile of v0, /device:TPU:8, one launch (start us, length us, event | category | flops | bytes accessed | tf_op | source)
XLA Modules:
  0.0 177.8 jit_solution(15432574918795712005)
XLA Ops:
  0.6 0.7 multiply_convert_fusion
  1.3 0.6 broadcast_in_dim.2
  1.9 11.3 %all-to-all-start.1 = ((bf16[32,128,2]{1,2,0:T(2,128)(2,1)}), bf16[32,128,2]{1,2,0:T(2,128)(2,1)S(1)}, u32[]{:S(2)}, u32[]{:S(2)}) async-start(bf16[32,128,2]{1,2,0:T(2,128)(2,1)} %broadcast_in_dim.2), calls=%async_computation.1 | async-start | bytes 32768 | tf_op jit(solution)/shard_map/all_to_all | solution.py:24
  13.3 4.6 %multiply_reduce_fusion = f32[2,6400]{1,0:T(2,128)S(1)} fusion(f32[2,6400,128]{2,1,0:T(8,128)} %param.3), kind=kLoop, calls=%fused_computation.1 | loop fusion | flops 3264000 | bytes 6604800 | tf_op jit(solution)/shard_map/reduce_sum | solution.py:34
  17.9 30.5 %psum.14 = f32[2,6400]{1,0:T(2,128)S(1)} all-reduce(f32[2,6400]{1,0:T(2,128)S(1)} %multiply_reduce_fusion), channel_id=1, replica_groups=mesh['ep'=8,'fsdp_0'=8,'fsdp_1'=4] {'fsdp_0'}, use_global_device_ids=true, to_apply=%region_1.0 | all-reduce | flops 12800 | bytes 102400 | tf_op jit(solution)/shard_map/psum | solution.py:12
  48.4 17.4 %psum.15 = f32[2,6400]{1,0:T(2,128)S(1)} all-reduce(f32[2,6400]{1,0:T(2,128)S(1)} %psum.14), channel_id=1, replica_groups=mesh['ep'=8,'fsdp_0'=8,'fsdp_1'=4] {'fsdp_1'}, use_global_device_ids=true, to_apply=%region_2.0 | all-reduce | flops 12800 | bytes 102400 | tf_op jit(solution)/shard_map/psum | solution.py:12
  65.8 0.1 sqrt.3
  65.9 4.7 %divide_convert_fusion = bf16[2,6400,128]{2,1,0:T(8,128)(2,1)S(1)} fusion(f32[2,6400,128]{2,1,0:T(8,128)} %param.3, f32[2,6400]{1,0:T(2,128)S(1)} %sqrt.3), kind=kLoop, calls=%fused_computation | loop fusion | flops 3276800 | bytes 9881600 | tf_op jit(solution)/shard_map/convert_element_type | solution.py:36
  70.6 27.9 %copy.10 = bf16[2,6400,128]{2,0,1:T(2,128)(2,1)} copy(bf16[2,6400,128]{2,1,0:T(8,128)(2,1)S(1)} %divide_convert_fusion) | data formatting | bytes 6553600 | tf_op jit(solution)/shard_map/convert_element_type | solution.py:36
  98.5 0.0 all-to-all-done.1
  98.5 5.7 %all-to-all-start = ((bf16[2,6400,128]{2,0,1:T(2,128)(2,1)}), bf16[2,6400,128]{2,0,1:T(2,128)(2,1)S(1)}, u32[]{:S(2)}, u32[]{:S(2)}) async-start(bf16[2,6400,128]{2,0,1:T(2,128)(2,1)} %copy.10), calls=%async_computation | async-start | bytes 6553600 | tf_op jit(solution)/shard_map/all_to_all | solution.py:37
  104.2 0.7 constant_dynamic-slice_fusion
  104.9 12.9 %all-gather = bf16[8,2,4096]{2,1,0:T(2,128)(2,1)S(1)} all-gather(bf16[1,2,4096]{2,1,0:T(2,128)(2,1)S(1)} %bitcast.13), channel_id=1, replica_groups=mesh['ep'=8,'fsdp_0'=8,'fsdp_1'=4] {'ep'}, dimensions={0}, use_global_device_ids=true | all-gather | bytes 147456 | tf_op jit(solution)/shard_map/all_gather | solution.py:43
  117.8 0.7 reshape.14
  118.5 50.5 %all-to-all-done = bf16[2,6400,128]{2,0,1:T(2,128)(2,1)S(1)} async-done(((bf16[2,6400,128]{2,0,1:T(2,128)(2,1)}), bf16[2,6400,128]{2,0,1:T(2,128)(2,1)S(1)}, u32[]{:S(2)}, u32[]{:S(2)}) %all-to-all-start) | async-done | bytes 3276832 | tf_op jit(solution)/shard_map/all_to_all | solution.py:37
  169.1 2.5 %copy.11 = bf16[2,200,32,128]{3,2,1,0:T(8,128)(2,1)} copy(bf16[2,200,32,128]{3,0,1,2:T(2,128)(2,1)S(1)} %bitcast.11) | data formatting | bytes 6553600 | tf_op jit(solution)/shard_map/all_to_all | solution.py:37
  171.6 6.2 %all_to_all.19 = bf16[2,200,4096]{2,1,0:T(8,128)(2,1)} reshape(bf16[2,200,32,128]{3,2,1,0:T(8,128)(2,1)} %copy.11) | data formatting | bytes 6553600 | tf_op jit(solution)/shard_map/all_to_all | solution.py:37
Async XLA Ops:
  1.9 96.6 %all-to-all-start.1 = ((bf16[32,128,2]{1,2,0:T(2,128)(2,1)}), bf16[32,128,2]{1,2,0:T(2,128)(2,1)S(1)}, u32[]{:S(2)}, u32[]{:S(2)}) async-start(bf16[32,128,2]{1,2,0:T(2,128)(2,1)} %broadcast_in_dim.2), calls=%async_computation.1 | async-start | bytes 32768 | tf_op jit(solution)/shard_map/all_to_all | solution.py:24
  98.5 70.6 %all-to-all-start = ((bf16[2,6400,128]{2,0,1:T(2,128)(2,1)}), bf16[2,6400,128]{2,0,1:T(2,128)(2,1)S(1)}, u32[]{:S(2)}, u32[]{:S(2)}) async-start(bf16[2,6400,128]{2,0,1:T(2,128)(2,1)} %copy.10), calls=%async_computation | async-start | bytes 6553600 | tf_op jit(solution)/shard_map/all_to_all | solution.py:37
where the time goes:
time: 178 us
  blocking collectives  60.9 us (34%)
  waiting for transfers between devices  50.5 us (28%)
  local copies, waits for them, and re-layouts  38.6 us (22%)
  starting transfers between devices  17 us (10%)
  other arithmetic  10 us (6%)
    all_to_all x1, waiting for transfers between devices, body(): lax.all_to_all(narrow_down, FSDP, split_axis=1, concat_axis=2, tiled=True)  50.5 us
    psum x2, blocking collectives, by_axis(): array = lax.psum(array, axis)  47.9 us
    convert_element_type x1, local copies, waits for them, and re-layouts, body(): narrow_down = (w_down / jnp.expand_dims(scale_down, 2)).astype(jnp.bfloat16)  27.9 us
    all_gather x1, blocking collectives, body(): serve_router = lax.all_gather(row_router, 'ep', axis=1, tiled=True)  12.9 us
    all_to_all x1, starting transfers between devices, copy_for_each(): lax.all_to_all(jnp.broadcast_to(array[None], (size, *array.shape)), axis,...  11.3 us
    all_to_all x2, local copies, waits for them, and re-layouts, body(): lax.all_to_all(narrow_down, FSDP, split_axis=1, concat_axis=2, tiled=True)  8.73 us
    all_to_all x1, starting transfers between devices, body(): lax.all_to_all(narrow_down, FSDP, split_axis=1, concat_axis=2, tiled=True)  5.7 us
    convert_element_type x1, other arithmetic, body(): narrow_down = (w_down / jnp.expand_dims(scale_down, 2)).astype(jnp.bfloat16)  4.71 us
  transfers between devices with their start and end apart: 2, of which 1 were waited for; matrix products, arithmetic and copies ran while one was open for 22% of the time, Pallas kernels for 0%

commit v1 on v0

--- a/solution.py
+++ b/solution.py
@@ -40,7 +40,16 @@
     )
     part_router = (router_weight * router_gain[:, None]).astype(jnp.bfloat16)
     row_router = gather_directly(part_router, FSDP, 0)
-    serve_router = lax.all_gather(row_router, "ep", axis=1, tiled=True)
+    ways = lax.axis_size("ep")
+    up = [(d, (d + 1) % ways) for d in range(ways)]
+    down = [(d, (d - 1) % ways) for d in range(ways)]
+    earlier, later = ([row_router], [row_router])
+    for _ in range(ways // 2):
+        earlier.append(lax.ppermute(earlier[-1], "ep", up))
+    for _ in range((ways - 1) // 2):
+        later.append(lax.ppermute(later[-1], "ep", down))
+    line = jnp.concatenate([*earlier[::-1], *later[1:]], axis=1)
+    serve_router = jnp.roll(line, (lax.axis_index("ep") - ways // 2) * row_router.shape[1], axis=1)
     return (serve_down, scale_down, serve_router)
 
 

time: 178 us -> 179 us (level)
  blocking collectives: 60.9 us -> 47.9 us
  starting transfers between devices: 17 us -> 22.2 us
  local copies, waits for them, and re-layouts: 38.6 us -> 43.2 us
  waiting for transfers between devices: 50.5 us -> 53.6 us
    all_gather x1 -> x0, blocking collectives: 12.9 us -> none  [body(): serve_router = lax.all_gather(row_router, 'ep', axis=1, tiled=True)]
    ppermute x0 -> x7, waiting for transfers between devices: none -> 5.68 us  [the longest x4 5.34 us: body(): earlier.append(lax.ppermute(earlier[-1], 'ep', up))]
    ppermute x0 -> x7, starting transfers between devices: none -> 5.21 us  [the longest x3 5.18 us: body(): later.append(lax.ppermute(later[-1], 'ep', down))]
    concatenate x0 -> x1, local copies, waits for them, and re-layouts: none -> 3.41 us  [body(): jnp.roll(line, (lax.axis_index('ep') - ways // 2) * row_router.shape[1],...]
    all_to_all x1, waiting for transfers between devices: 50.5 us -> 48 us  [body(): lax.all_to_all(narrow_down, FSDP, split_axis=1, concat_axis=2, tiled=True)]
  transfers between devices with their start and end apart: 2 -> 9, of which waited for: 1 -> 6; matrix products, arithmetic and copies ran while one was open for 22% -> 24% of each run, Pallas kernels for 0% -> 0%
where the time goes in v1:
time: 179 us; the launch traced here: 178 us
  waiting for transfers between devices  53.6 us (30%)
  blocking collectives  47.9 us (27%)
  local copies, waits for them, and re-layouts  43.2 us (24%)
  starting transfers between devices  22.2 us (12%)
  other arithmetic  10 us (6%)
    all_to_all x1, waiting for transfers between devices, body(): lax.all_to_all(narrow_down, FSDP, split_axis=1, concat_axis=2, tiled=True)  48 us
    psum x2, blocking collectives, by_axis(): array = lax.psum(array, axis)  47.9 us
    convert_element_type x1, local copies, waits for them, and re-layouts, body(): narrow_down = (w_down / jnp.expand_dims(scale_down, 2)).astype(jnp.bfloat16)  27.9 us
    all_to_all x1, starting transfers between devices, copy_for_each(): lax.all_to_all(jnp.broadcast_to(array[None], (size, *array.shape)), axis,...  11.3 us
    all_to_all x2, local copies, waits for them, and re-layouts, body(): lax.all_to_all(narrow_down, FSDP, split_axis=1, concat_axis=2, tiled=True)  8.74 us
    all_to_all x1, starting transfers between devices, body(): lax.all_to_all(narrow_down, FSDP, split_axis=1, concat_axis=2, tiled=True)  5.7 us
    ppermute x4, waiting for transfers between devices, body(): earlier.append(lax.ppermute(earlier[-1], 'ep', up))  5.34 us
    ppermute x3, starting transfers between devices, body(): later.append(lax.ppermute(later[-1], 'ep', down))  5.18 us
  transfers between devices with their start and end apart: 9, of which 6 were waited for; matrix products, arithmetic and copies ran while one was open for 24% of the time, Pallas kernels for 0%

profile of v1, /device:TPU:8, one launch (start us, length us, event | category | flops | bytes accessed | tf_op | source)
XLA Modules:
  0.0 177.8 jit_solution(1075704525552873363)
XLA Ops:
  0.6 0.7 multiply_convert_fusion
  1.3 0.6 broadcast_in_dim.2
  1.9 11.3 %all-to-all-start.1 = ((bf16[32,128,2]{1,2,0:T(2,128)(2,1)}), bf16[32,128,2]{1,2,0:T(2,128)(2,1)S(1)}, u32[]{:S(2)}, u32[]{:S(2)}) async-start(bf16[32,128,2]{1,2,0:T(2,128)(2,1)} %broadcast_in_dim.2), calls=%async_computation.1 | async-start | bytes 32768 | tf_op jit(solution)/shard_map/all_to_all | solution.py:24
  13.3 4.6 %multiply_reduce_fusion = f32[2,6400]{1,0:T(2,128)S(1)} fusion(f32[2,6400,128]{2,1,0:T(8,128)} %param.3), kind=kLoop, calls=%fused_computation.1 | loop fusion | flops 3264000 | bytes 6604800 | tf_op jit(solution)/shard_map/reduce_sum | solution.py:34
  17.9 30.5 %psum.14 = f32[2,6400]{1,0:T(2,128)S(1)} all-reduce(f32[2,6400]{1,0:T(2,128)S(1)} %multiply_reduce_fusion), channel_id=1, replica_groups=mesh['ep'=8,'fsdp_0'=8,'fsdp_1'=4] {'fsdp_0'}, use_global_device_ids=true, to_apply=%region_1.0 | all-reduce | flops 12800 | bytes 102400 | tf_op jit(solution)/shard_map/psum | solution.py:12
  48.4 17.4 %psum.15 = f32[2,6400]{1,0:T(2,128)S(1)} all-reduce(f32[2,6400]{1,0:T(2,128)S(1)} %psum.14), channel_id=1, replica_groups=mesh['ep'=8,'fsdp_0'=8,'fsdp_1'=4] {'fsdp_1'}, use_global_device_ids=true, to_apply=%region_2.0 | all-reduce | flops 12800 | bytes 102400 | tf_op jit(solution)/shard_map/psum | solution.py:12
  65.9 4.7 %divide_convert_fusion = bf16[2,6400,128]{2,1,0:T(8,128)(2,1)S(1)} fusion(f32[2,6400,128]{2,1,0:T(8,128)} %param.3, f32[2,6400]{1,0:T(2,128)S(1)} %sqrt.3), kind=kLoop, calls=%fused_computation | loop fusion | flops 3276800 | bytes 9881600 | tf_op jit(solution)/shard_map/convert_element_type | solution.py:36
  70.6 27.9 %copy.10 = bf16[2,6400,128]{2,0,1:T(2,128)(2,1)} copy(bf16[2,6400,128]{2,1,0:T(8,128)(2,1)S(1)} %divide_convert_fusion) | data formatting | bytes 6553600 | tf_op jit(solution)/shard_map/convert_element_type | solution.py:36
  98.5 5.7 %all-to-all-start = ((bf16[2,6400,128]{2,0,1:T(2,128)(2,1)}), bf16[2,6400,128]{2,0,1:T(2,128)(2,1)S(1)}, u32[]{:S(2)}, u32[]{:S(2)}) async-start(bf16[2,6400,128]{2,0,1:T(2,128)(2,1)} %copy.10), calls=%async_computation | async-start | bytes 6553600 | tf_op jit(solution)/shard_map/all_to_all | solution.py:37
  104.2 1.7 collective-permute-start.4
  106.0 1.4 collective-permute-done
  107.4 0.6 copy-done
  108.0 1.4 collective-permute-start.5
  109.4 1.1 collective-permute-done.1
  110.9 2.0 %collective-permute-start.6 = (bf16[4096,2]{0,1:T(2,128)(2,1)S(1)}, bf16[4096,2]{0,1:T(2,128)(2,1)S(1)}, u32[]{:S(2)}, u32[]{:S(2)}) collective-permute-start(bf16[4096,2]{0,1:T(2,128)(2,1)S(1)} %collective-permute-done.5), channel_id=1, source_target_pairs={{0,224},{32,0},{64,32},{96,64},{128,96},{160,128},{192,160},{224,1... | collective-permute-start | bytes 49160 | tf_op jit(solution)/shard_map/ppermute | solution.py:50
  112.9 0.8 collective-permute-done.2
  113.7 0.7 constant_dynamic-slice_fusion.1
  114.4 0.6 copy-done.5
  115.0 2.0 %collective-permute-done.3 = bf16[4096,2]{0,1:T(2,128)(2,1)} collective-permute-done((bf16[4096,2]{0,1:T(2,128)(2,1)S(1)}, bf16[4096,2]{0,1:T(2,128)(2,1)}, u32[]{:S(2)}, u32[]{:S(2)}) %collective-permute-start.3) | collective-permute-done | bytes 16416 | tf_op jit(solution)/shard_map/ppermute | solution.py:48
  117.0 3.4 %concatenate.6 = bf16[4096,32]{0,1:T(8,128)(2,1)S(1)} concatenate(bf16[4096,2]{0,1:T(2,128)(2,1)} %collective-permute-done.3, bf16[4096,2]{0,1:T(2,128)(2,1)} %copy-done.4, bf16[4096,2]{0,1:T(2,128)(2,1)} %copy-done.2, bf16[4096,2]{0,1:T(2,128)(2,1)} %copy-done, bf16[4096,2]{0,1:T(2,128)(2,1)S(1)} %bitcast.9, bf16[4096,2]{0,1:T(2,128)(2,1)} %copy-done.1, ...), dimensions={1} | concatenate | bytes 524288 | tf_op jit(solution)/shard_map/jit(_roll_dynamic)/concatenate | solution.py:52
  120.4 0.7 constant_dynamic-slice_fusion
  121.1 48.0 %all-to-all-done = bf16[2,6400,128]{2,0,1:T(2,128)(2,1)S(1)} async-done(((bf16[2,6400,128]{2,0,1:T(2,128)(2,1)}), bf16[2,6400,128]{2,0,1:T(2,128)(2,1)S(1)}, u32[]{:S(2)}, u32[]{:S(2)}) %all-to-all-start) | async-done | bytes 3276832 | tf_op jit(solution)/shard_map/all_to_all | solution.py:37
  169.1 2.5 %copy.11 = bf16[2,200,32,128]{3,2,1,0:T(8,128)(2,1)} copy(bf16[2,200,32,128]{3,0,1,2:T(2,128)(2,1)S(1)} %bitcast.6) | data formatting | bytes 6553600 | tf_op jit(solution)/shard_map/all_to_all | solution.py:37
  171.6 6.2 %all_to_all.19 = bf16[2,200,4096]{2,1,0:T(8,128)(2,1)} reshape(bf16[2,200,32,128]{3,2,1,0:T(8,128)(2,1)} %copy.11) | data formatting | bytes 6553600 | tf_op jit(solution)/shard_map/all_to_all | solution.py:37
  (19 shorter events, 0.4 us)
Async XLA Ops:
  1.9 96.6 %all-to-all-start.1 = ((bf16[32,128,2]{1,2,0:T(2,128)(2,1)}), bf16[32,128,2]{1,2,0:T(2,128)(2,1)S(1)}, u32[]{:S(2)}, u32[]{:S(2)}) async-start(bf16[32,128,2]{1,2,0:T(2,128)(2,1)} %broadcast_in_dim.2), calls=%async_computation.1 | async-start | bytes 32768 | tf_op jit(solution)/shard_map/all_to_all | solution.py:24
  98.5 70.6 %all-to-all-start = ((bf16[2,6400,128]{2,0,1:T(2,128)(2,1)}), bf16[2,6400,128]{2,0,1:T(2,128)(2,1)S(1)}, u32[]{:S(2)}, u32[]{:S(2)}) async-start(bf16[2,6400,128]{2,0,1:T(2,128)(2,1)} %copy.10), calls=%async_computation | async-start | bytes 6553600 | tf_op jit(solution)/shard_map/all_to_all | solution.py:37
  104.2 3.2 %collective-permute-start = (bf16[4096,2]{0,1:T(2,128)(2,1)S(1)}, bf16[4096,2]{0,1:T(2,128)(2,1)S(1)}, u32[]{:S(2)}, u32[]{:S(2)}) collective-permute-start(bf16[4096,2]{0,1:T(2,128)(2,1)S(1)} %bitcast.7), channel_id=1, source_target_pairs={{0,32},{32,64},{64,96},{96,128},{128,160},{160,192},{192,224},{224... | collective-permute-start | bytes 49160 | tf_op jit(solution)/shard_map/ppermute | solution.py:48
  104.2 3.2 %collective-permute-start.4 = (bf16[4096,2]{0,1:T(2,128)(2,1)S(1)}, bf16[4096,2]{0,1:T(2,128)(2,1)S(1)}, u32[]{:S(2)}, u32[]{:S(2)}) collective-permute-start(bf16[4096,2]{0,1:T(2,128)(2,1)S(1)} %bitcast.8), channel_id=1, source_target_pairs={{0,224},{32,0},{64,32},{96,64},{128,96},{160,128},{192,160},{224,1... | collective-permute-start | bytes 49160 | tf_op jit(solution)/shard_map/ppermute | solution.py:50
  107.4 0.6 copy-start
  107.4 3.2 %collective-permute-start.1 = (bf16[4096,2]{0,1:T(2,128)(2,1)S(1)}, bf16[4096,2]{0,1:T(2,128)(2,1)S(1)}, u32[]{:S(2)}, u32[]{:S(2)}) collective-permute-start(bf16[4096,2]{0,1:T(2,128)(2,1)S(1)} %collective-permute-done), channel_id=1, source_target_pairs={{0,32},{32,64},{64,96},{96,128},{128,160},{160,192},{192,224},{224... | collective-permute-start | bytes 49160 | tf_op jit(solution)/shard_map/ppermute | solution.py:48
  108.0 6.4 %copy-start.1 = (bf16[4096,2]{0,1:T(2,128)(2,1)}, bf16[4096,2]{0,1:T(2,128)(2,1)S(1)}, u32[]{:S(2)}) copy-start(bf16[4096,2]{0,1:T(2,128)(2,1)S(1)} %collective-permute-done.4) | copy-start | bytes 49156
  108.0 2.9 %collective-permute-start.5 = (bf16[4096,2]{0,1:T(2,128)(2,1)S(1)}, bf16[4096,2]{0,1:T(2,128)(2,1)S(1)}, u32[]{:S(2)}, u32[]{:S(2)}) collective-permute-start(bf16[4096,2]{0,1:T(2,128)(2,1)S(1)} %collective-permute-done.4), channel_id=1, source_target_pairs={{0,224},{32,0},{64,32},{96,64},{128,96},{160,128},{192,160},{224,1... | collective-permute-start | bytes 49160 | tf_op jit(solution)/shard_map/ppermute | solution.py:50
  110.6 3.8 %copy-start.2 = (bf16[4096,2]{0,1:T(2,128)(2,1)}, bf16[4096,2]{0,1:T(2,128)(2,1)S(1)}, u32[]{:S(2)}) copy-start(bf16[4096,2]{0,1:T(2,128)(2,1)S(1)} %collective-permute-done.1) | copy-start | bytes 49156
  110.6 3.2 %collective-permute-start.2 = (bf16[4096,2]{0,1:T(2,128)(2,1)S(1)}, bf16[4096,2]{0,1:T(2,128)(2,1)S(1)}, u32[]{:S(2)}, u32[]{:S(2)}) collective-permute-start(bf16[4096,2]{0,1:T(2,128)(2,1)S(1)} %collective-permute-done.1), channel_id=1, source_target_pairs={{0,32},{32,64},{64,96},{96,128},{128,160},{160,192},{192,224},{224... | collective-permute-start | bytes 49160 | tf_op jit(solution)/shard_map/ppermute | solution.py:48
  110.9 3.5 %copy-start.3 = (bf16[4096,2]{0,1:T(2,128)(2,1)}, bf16[4096,2]{0,1:T(2,128)(2,1)S(1)}, u32[]{:S(2)}) copy-start(bf16[4096,2]{0,1:T(2,128)(2,1)S(1)} %collective-permute-done.5) | copy-start | bytes 49156
  110.9 3.5 %collective-permute-start.6 = (bf16[4096,2]{0,1:T(2,128)(2,1)S(1)}, bf16[4096,2]{0,1:T(2,128)(2,1)S(1)}, u32[]{:S(2)}, u32[]{:S(2)}) collective-permute-start(bf16[4096,2]{0,1:T(2,128)(2,1)S(1)} %collective-permute-done.5), channel_id=1, source_target_pairs={{0,224},{32,0},{64,32},{96,64},{128,96},{160,128},{192,160},{224,1... | collective-permute-start | bytes 49160 | tf_op jit(solution)/shard_map/ppermute | solution.py:50
  113.7 0.7 copy-start.4
  113.7 3.3 %collective-permute-start.3 = (bf16[4096,2]{0,1:T(2,128)(2,1)S(1)}, bf16[4096,2]{0,1:T(2,128)(2,1)}, u32[]{:S(2)}, u32[]{:S(2)}) collective-permute-start(bf16[4096,2]{0,1:T(2,128)(2,1)S(1)} %collective-permute-done.2), channel_id=1, source_target_pairs={{0,32},{32,64},{64,96},{96,128},{128,160},{160,192},{192,224},{224... | collective-permute-start | bytes 49160 | tf_op jit(solution)/shard_map/ppermute | solution.py:48
  114.4 0.6 copy-start.5
